TPU v7x, 32 devices: a whole 2x2x4 slice. The times are simulated.
32 devices in a mesh: rows: 8 (over z, x), cols: 4 (over y, core).
Axes of the slice: x: 2, y: 2, z: 4, core: 2. Of those that a mesh axis runs over, the one named last changes fastest.
Arguments:
- basis: float32 [8192, 4096], P('rows', 'cols'), may hold values from -119.66257 to 119.66257, as said below
- block: float32 [8192, 512], P('rows', 'cols'), may hold values from -1800 to 1800
Outputs:
- ortho: float32 [8192, 512], P('rows', 'cols')
- factors: float32 [4, 128, 128], P('cols')
Inputs may be any that keep to these rules, and one draw needn't show every extreme that they name: Under the inner product (sum over rows divided by 8192) the basis columns have squared norms between 0.6 and 1.9, and inner products of distinct basis columns are at most 0.05 in magnitude.
All inputs are finite; a program needn't handle non-finite values.
Results may differ from a plain program's by a relative error of at most 0.000076.
Values sent between devices are 32-bit elements; how exact they have to be, the bound alone decides.
No kernel may reach another device: no remote copies, remote signals or barrier semaphores. Data moves between devices by JAX's collectives and lax.ppermute only.
A program may use at most 64 MiB of HBM per device.

v0:
```python
import jax
import jax.numpy as jnp
from jax import lax
from jax.sharding import PartitionSpec as P

BLK = 128


def solve_block(lower_factor, vectors):
    return jax.scipy.linalg.solve_triangular(lower_factor, vectors, lower=True)


def body(basis, block):
    highest = lax.Precision.HIGHEST
    local_rows = basis.shape[0]
    inverse = 1.0 / (local_rows * lax.axis_size("rows"))
    width = block.shape[1]
    column_index = lax.axis_index("cols")

    def project(piece):
        return (
            lax.dot_general(
                basis,
                piece,
                (((0,), (0,)), ((), ())),
                precision=highest,
                preferred_element_type=jnp.float32,
            )
            * inverse
        )

    def expand(coef):
        return jnp.dot(basis, coef, precision=highest, preferred_element_type=jnp.float32)

    terms_one = project(lax.all_gather(block, "cols", axis=1, tiled=True))
    coef_one = lax.psum(terms_one, "rows")
    placed = lax.dynamic_update_slice_in_dim(
        jnp.zeros((local_rows, coef_one.shape[1]), jnp.float32), block, column_index * width, 1
    )
    first_whole = lax.psum(placed - expand(coef_one), "cols")
    terms_two = project(first_whole)
    first = lax.dynamic_slice_in_dim(first_whole, column_index * width, width, 1)
    coef_two = lax.psum(terms_two, "rows")
    second = first - lax.psum_scatter(expand(coef_two), "cols", scatter_dimension=1, tiled=True)
    blocks = width // BLK
    pieces = second.reshape(local_rows, blocks, BLK)
    gram = jnp.einsum("mbi,mbj->bij", pieces, pieces, precision=highest) * inverse
    gram = lax.psum(gram, "rows")
    lower_factor = jnp.linalg.cholesky(gram)
    solved = jax.vmap(solve_block)(lower_factor, jnp.transpose(pieces, (1, 2, 0)))
    ortho = jnp.transpose(solved, (2, 0, 1)).reshape(local_rows, width)
    return (ortho, jnp.transpose(lower_factor, (0, 2, 1)))


def solution(mesh):
    placed = (P("rows", "cols"), P("rows", "cols"))
    return jax.shard_map(
        body,
        mesh=mesh,
        in_specs=placed,
        out_specs=(P("rows", "cols"), P("cols", None, None)),
        check_vma=False,
    )
```

profile of v0, /device:TPU:0, one launch (start us, length us, event | category | flops | bytes accessed | tf_op | source)
XLA Modules:
  0.0 476.0 jit_solution(7517272405939530119)
XLA Ops:
  7.2 0.0 all-gather.2.cloned.1.call-start
  7.2 0.7 all-gather.2.cloned.1.call-update
  7.9 0.0 all-reduce.5.cloned.1.call-start
  7.9 27.2 %all-gather.2.cloned.1.call-done = f32[1024,512]{1,0:T(8,128)} async-done(((f32[1024,128]{1,0:T(8,128)}), f32[1024,512]{1,0:T(8,128)}) %all-gather.2.cloned.1.call-update) | async-done | bytes 2097168 | tf_op jit(solution)/shard_map/all_gather | solution.py:35
  35.1 10.2 %convolution_multiply_fusion = f32[1024,512]{1,0:T(8,128)} fusion(f32[1024,1024]{1,0:T(8,128)} %param.2, f32[1024,512]{1,0:T(8,128)} %all-gather.2.cloned.1.call-done), kind=kOutput, calls=%fused_computation.3 | convolution fusion | flops 6442975232 | bytes 8388608 | tf_op jit(solution)/shard_map/dot_general | solution.py:22
  45.3 0.0 copy-start.1
  45.3 0.0 all-reduce.5.cloned.1.call-update
  45.3 0.0 all-reduce.7.cloned.1.call-start
  45.4 1.0 copy-done.1
  46.3 0.2 copy.4
  46.5 0.2 broadcast_in_dim.7
  46.8 0.1 constant_dynamic-update-slice_fusion
  46.8 100.9 %all-reduce.5.cloned.1.call-done = f32[1024,512]{1,0:T(8,128)} async-done(((f32[1024,512]{1,0:T(8,128)}), f32[1024,512]{1,0:T(8,128)}) %all-reduce.5.cloned.1.call-update) | async-done | bytes 2097168 | tf_op jit(solution)/shard_map/psum | solution.py:36
  147.8 16.7 %bitcast_subtract_fusion = f32[1024,512]{0,1:T(8,128)} fusion(f32[1024,512]{0,1:T(8,128)S(1)} %constant_dynamic-update-slice_fusion, f32[1024,512]{1,0:T(8,128)} %all-reduce.5.cloned.1.call-done, f32[1024,1024]{1,0:T(8,128)} %param.2), kind=kOutput, calls=%fused_computation | convolution fusion | flops 6442975232 | bytes 10485760 | tf_op jit(solution)/shard_map/dot_general | solution.py:33
  164.5 0.0 all-reduce.7.cloned.1.call-update
  164.5 0.2 all-reduce.9.cloned.1.call-start
  164.7 50.6 %all-reduce.7.cloned.1.call-done = f32[1024,512]{0,1:T(8,128)} async-done(((f32[1024,512]{0,1:T(8,128)}), f32[1024,512]{0,1:T(8,128)}) %all-reduce.7.cloned.1.call-update) | async-done | bytes 2097168 | tf_op jit(solution)/shard_map/psum | solution.py:40
  215.3 10.2 %multiply_bitcast_fusion = f32[1024,512]{0,1:T(8,128)} fusion(f32[1024,512]{0,1:T(8,128)} %all-reduce.7.cloned.1.call-done, f32[1024,1024]{1,0:T(8,128)} %param.2), kind=kOutput, calls=%fused_computation.1 | convolution fusion | flops 6442975232 | bytes 8388608 | tf_op jit(solution)/shard_map/dot_general | solution.py:22
  225.6 0.0 all-reduce.9.cloned.1.call-update
  225.6 0.0 reduce-scatter.2.cloned.1.call-start
  225.6 102.5 %all-reduce.9.cloned.1.call-done = f32[1024,512]{0,1:T(8,128)} async-done(((f32[1024,512]{0,1:T(8,128)}), f32[1024,512]{0,1:T(8,128)}) %all-reduce.9.cloned.1.call-update) | async-done | bytes 2097168 | tf_op jit(solution)/shard_map/psum | solution.py:43
  328.1 10.3 %convolution_bitcast_fusion = f32[1024,512]{0,1:T(8,128)} fusion(f32[1024,512]{0,1:T(8,128)} %all-reduce.9.cloned.1.call-done, f32[1024,1024]{1,0:T(8,128)} %param.2), kind=kOutput, calls=%fused_computation.2 | convolution fusion | flops 6442450944 | bytes 8388608 | tf_op jit(solution)/shard_map/dot_general | solution.py:33
  338.4 0.0 copy-start
  338.4 0.0 reduce-scatter.2.cloned.1.call-update
  338.4 0.3 all-reduce.11.cloned.1.call-start
  338.7 30.3 %reduce-scatter.2.cloned.1.call-done = f32[1024,128]{0,1:T(8,128)} async-done(((f32[1024,512]{0,1:T(8,128)}), f32[1024,128]{0,1:T(8,128)}) %reduce-scatter.2.cloned.1.call-update) | async-done | bytes 524304 | tf_op jit(solution)/shard_map/reduce_scatter | solution.py:44
  369.0 0.0 copy-done
  369.0 0.0 copy-start.2
  369.0 2.5 fusion
  371.5 0.0 all-reduce.11.cloned.1.call-update
  371.5 70.6 %all-reduce.11.cloned.1.call-done = f32[1,128,128]{1,2,0:T(8,128)} async-done(((f32[1,128,128]{1,2,0:T(8,128)}), f32[1,128,128]{1,2,0:T(8,128)}) %all-reduce.11.cloned.1.call-update) | async-done | bytes 65552 | tf_op jit(solution)/shard_map/psum | solution.py:48
  442.2 0.9 copy.6
  443.1 0.9 fusion.3
  444.0 11.7 %custom-call.8 = f32[1,128,128]{2,1,0:T(8,128)S(1)} custom-call(f32[1,128,128]{2,1,0:T(8,128)S(1)} %fusion.3), custom_call_target="Cholesky" | custom-call | tf_op jit(solution)/shard_map/jit(cholesky)/cholesky | solution.py:49
  455.7 0.6 compare_reduce_fusion
  456.4 0.7 fusion.4
  457.0 9.8 %custom-call.9 = f32[1,1,128,128]{2,3,1,0:T(8,128)S(1)} custom-call(f32[1,1,128,128]{3,2,1,0:T(8,128)S(1)} %get-tuple-element.5), custom_call_target="InvertDiagBlocksLowerTriangular" | custom-call | tf_op jit(solution)/shard_map/vmap(jit(_solve_triangular))/triangular_solve | solution.py:10
  466.8 0.0 copy-done.2
  466.8 0.6 convolution_bitcast_fusion.1
  467.5 1.0 copy.7
  468.5 0.7 copy.8
  (1 shorter events, 0.0 us)
Async XLA Ops:
  7.2 27.9 %all-gather.2.cloned.1.call-start = ((), (), s32[]{:S(2)}) async-start(), calls=%async_computation.1 | async-start | bytes 2621440 | tf_op jit(solution)/shard_map/all_gather | solution.py:35
  7.9 139.9 %all-reduce.5.cloned.1.call-start = ((), (), s32[]{:S(2)}) async-start(), calls=%async_computation.2 | async-start | bytes 4194304 | tf_op jit(solution)/shard_map/psum | solution.py:36
  45.3 1.0 copy-start.1
  45.3 170.0 %all-reduce.7.cloned.1.call-start = ((), (), s32[]{:S(2)}) async-start(), calls=%async_computation.3 | async-start | bytes 4194304 | tf_op jit(solution)/shard_map/psum | solution.py:40
  164.5 163.6 %all-reduce.9.cloned.1.call-start = ((), (), s32[]{:S(2)}) async-start(), calls=%async_computation.4 | async-start | bytes 4194304 | tf_op jit(solution)/shard_map/psum | solution.py:43
  225.6 143.4 %reduce-scatter.2.cloned.1.call-start = ((), (), s32[]{:S(2)}) async-start(), calls=%async_computation.5 | async-start | bytes 2621440 | tf_op jit(solution)/shard_map/reduce_scatter | solution.py:44
  338.4 30.6 %copy-start = (f32[1024,512]{0,1:T(8,128)S(1)}, f32[1024,512]{0,1:T(8,128)}, u32[]{:S(2)}) copy-start(f32[1024,512]{0,1:T(8,128)} %all-reduce.7.cloned.1.call-done) | copy-start | bytes 6291460
  338.4 103.8 %all-reduce.11.cloned.1.call-start = ((), (), s32[]{:S(2)}) async-start(), calls=%async_computation.6 | async-start | bytes 131072 | tf_op jit(solution)/shard_map/psum | solution.py:48
  369.0 97.8 %copy-start.2 = (f32[1024,128]{0,1:T(8,128)S(1)}, f32[1024,128]{0,1:T(8,128)}, u32[]{:S(2)}) copy-start(f32[1024,128]{0,1:T(8,128)} %reduce-scatter.2.cloned.1.call-done) | copy-start | bytes 1572868
Sparse Core Ops, SparseCore 0:
  9.5 25.5 all-gather.1
  45.4 102.3 all-reduce.4
  164.6 50.6 all-reduce.6
  225.7 102.3 all-reduce.8
  338.5 30.4 reduce-scatter.1
  372.9 69.2 all-reduce.10
where the time goes:
time: 476 us
  waiting for transfers between devices  383 us (80%)
  matrix products  50.5 us (11%)
  other arithmetic  23.7 us (5%)
  between operations  14.2 us (3%)
    psum x1, waiting for transfers between devices, body(): coef_two = lax.psum(terms_two, 'rows')  102 us
    psum x1, waiting for transfers between devices, body(): coef_one = lax.psum(terms_one, 'rows')  101 us
    psum x1, waiting for transfers between devices, body(): gram = lax.psum(gram, 'rows')  70.6 us
    psum x1, waiting for transfers between devices, body(): first_whole = lax.psum(placed - expand(coef_one), 'cols')  50.6 us
    reduce_scatter x1, waiting for transfers between devices, body(): lax.psum_scatter(expand(coef_two), 'cols', scatter_dimension=1, tiled=True)  30.3 us
    all_gather x1, waiting for transfers between devices, body(): terms_one = project(lax.all_gather(block, 'cols', axis=1, tiled=True))  27.2 us
    dot_general x2, matrix products, expand(): jnp.dot(basis, coef, precision=highest, preferred_element_type=jnp.float32)  27 us
    dot_general x2, matrix products, project(): lax.dot_general(basis, piece, (((0,), (0,)), ((), ())), precision=highest...  20.4 us
  transfers between devices with their start and end apart: 6, of which 6 were waited for; matrix products, arithmetic and copies ran while one was open for 0% of the time, Pallas kernels for 0%

commit v1 on v0

--- a/solution.py
+++ b/solution.py
@@ -2,6 +2,7 @@
 import jax.numpy as jnp
 from jax import lax
 from jax.sharding import PartitionSpec as P
+from jax.lax import axis_size, ppermute
 
 BLK = 128
 
@@ -11,6 +12,14 @@
 
 
 def body(basis, block):
+
+    def _read_inputs(unit):
+        q_n = axis_size("rows")
+        p_next = unit
+        for c in [[(m, m ^ rr) for m in range(q_n)] for rr in (1, 2, 4, 8, 16) if rr < q_n]:
+            p_next = p_next + ppermute(p_next, "rows", c)
+        return p_next
+
     highest = lax.Precision.HIGHEST
     local_rows = basis.shape[0]
     inverse = 1.0 / (local_rows * lax.axis_size("rows"))
@@ -33,7 +42,7 @@
         return jnp.dot(basis, coef, precision=highest, preferred_element_type=jnp.float32)
 
     terms_one = project(lax.all_gather(block, "cols", axis=1, tiled=True))
-    coef_one = lax.psum(terms_one, "rows")
+    coef_one = _read_inputs(terms_one)
     placed = lax.dynamic_update_slice_in_dim(
         jnp.zeros((local_rows, coef_one.shape[1]), jnp.float32), block, column_index * width, 1
     )

time: 476 us -> 561 us (1.18)
  waiting for transfers between devices: 383 us -> 463 us
    ppermute x0 -> x3, waiting for transfers between devices: none -> 181 us  [_read_inputs(): p_next = p_next + ppermute(p_next, 'rows', c)]
    psum x1 -> x0, waiting for transfers between devices: 101 us -> none  [body(): coef_one = lax.psum(terms_one, 'rows')]
  transfers between devices with their start and end apart: 6 -> 8, of which waited for: 6 -> 8; matrix products, arithmetic and copies ran while one was open for 0% -> 0% of each run, Pallas kernels for 0% -> 0%
where the time goes in v1:
time: 561 us
  waiting for transfers between devices  463 us (83%)
  matrix products  49.6 us (9%)
  other arithmetic  24.7 us (4%)
  between operations  13.9 us (2%)
  starting transfers between devices  6.16 us (1%)
    ppermute x3, waiting for transfers between devices, _read_inputs(): p_next = p_next + ppermute(p_next, 'rows', c)  181 us
    psum x1, waiting for transfers between devices, body(): coef_two = lax.psum(terms_two, 'rows')  102 us
    psum x1, waiting for transfers between devices, body(): gram = lax.psum(gram, 'rows')  70.6 us
    psum x1, waiting for transfers between devices, body(): first_whole = lax.psum(placed - expand(coef_one), 'cols')  51.3 us
    reduce_scatter x1, waiting for transfers between devices, body(): lax.psum_scatter(expand(coef_two), 'cols', scatter_dimension=1, tiled=True)  30.3 us
    all_gather x1, waiting for transfers between devices, body(): terms_one = project(lax.all_gather(block, 'cols', axis=1, tiled=True))  27.2 us
    dot_general x2, matrix products, expand(): jnp.dot(basis, coef, precision=highest, preferred_element_type=jnp.float32)  27 us
    dot_general x2, matrix products, project(): lax.dot_general(basis, piece, (((0,), (0,)), ((), ())), precision=highest...  19.5 us
  transfers between devices with their start and end apart: 8, of which 8 were waited for; matrix products, arithmetic and copies ran while one was open for 0% of the time, Pallas kernels for 0%

profile of v1, /device:TPU:0, one launch (start us, length us, event | category | flops | bytes accessed | tf_op | source)
XLA Modules:
  0.0 560.9 jit_solution(2306049510241651862)
XLA Ops:
  7.2 0.0 all-gather.2.cloned.1.call-start
  7.2 0.7 all-gather.2.cloned.1.call-update
  7.9 0.0 all-reduce.4.cloned.1.call-start
  7.9 27.2 %all-gather.2.cloned.1.call-done = f32[1024,512]{1,0:T(8,128)} async-done(((f32[1024,128]{1,0:T(8,128)}), f32[1024,512]{1,0:T(8,128)}) %all-gather.2.cloned.1.call-update) | async-done | bytes 2097168 | tf_op jit(solution)/shard_map/all_gather | solution.py:44
  35.1 9.2 %convolution_multiply_fusion = f32[1024,512]{1,0:T(8,128)S(1)} fusion(f32[1024,1024]{1,0:T(8,128)} %param.2, f32[1024,512]{1,0:T(8,128)} %all-gather.2.cloned.1.call-done), kind=kOutput, calls=%fused_computation.5 | convolution fusion | flops 6442975232 | bytes 8388608 | tf_op jit(solution)/shard_map/dot_general | solution.py:31
  44.3 1.5 collective-permute-start
  45.9 46.3 %collective-permute-done = f32[1024,512]{1,0:T(8,128)S(1)} collective-permute-done((f32[1024,512]{1,0:T(8,128)S(1)}, f32[1024,512]{1,0:T(8,128)S(1)}, u32[]{:S(2)}, u32[]{:S(2)}) %collective-permute-start) | collective-permute-done | bytes 2097184 | tf_op jit(solution)/shard_map/ppermute | solution.py:20
  92.2 0.5 add.34
  92.7 0.0 copy-start.1
  92.7 1.6 collective-permute-start.1
  94.2 45.4 %collective-permute-done.1 = f32[1024,512]{1,0:T(8,128)S(1)} collective-permute-done((f32[1024,512]{1,0:T(8,128)S(1)}, f32[1024,512]{1,0:T(8,128)S(1)}, u32[]{:S(2)}, u32[]{:S(2)}) %collective-permute-start.1) | collective-permute-done | bytes 2097184 | tf_op jit(solution)/shard_map/ppermute | solution.py:20
  139.7 0.5 add.35
  140.1 2.5 collective-permute-start.2
  142.6 0.0 copy-done.1
  142.6 0.2 copy.4
  142.8 0.2 broadcast_in_dim.7
  143.1 0.1 constant_dynamic-update-slice_fusion
  143.1 89.1 %collective-permute-done.2 = f32[1024,512]{1,0:T(8,128)} collective-permute-done((f32[1024,512]{1,0:T(8,128)S(1)}, f32[1024,512]{1,0:T(8,128)}, u32[]{:S(2)}, u32[]{:S(2)}) %collective-permute-start.2) | collective-permute-done | bytes 2097184 | tf_op jit(solution)/shard_map/ppermute | solution.py:20
  232.2 16.7 %bitcast_subtract_fusion = f32[1024,512]{0,1:T(8,128)} fusion(f32[1024,512]{0,1:T(8,128)S(1)} %constant_dynamic-update-slice_fusion, f32[1024,1024]{1,0:T(8,128)} %param.2, f32[1024,512]{1,0:T(8,128)S(1)} %add.35, f32[1024,512]{1,0:T(8,128)} %collective-permute-done.2), kind=kOutput, calls=%fused_computation | convolution fusion | flops 6443499520 | bytes 12582912 | tf_op jit(solution)/shard_map/dot_general | solution.py:42
  248.9 0.0 all-reduce.4.cloned.1.call-update
  248.9 0.2 all-reduce.6.cloned.1.call-start
  249.2 51.3 %all-reduce.4.cloned.1.call-done = f32[1024,512]{0,1:T(8,128)} async-done(((f32[1024,512]{0,1:T(8,128)}), f32[1024,512]{0,1:T(8,128)}) %all-reduce.4.cloned.1.call-update) | async-done | bytes 2097168 | tf_op jit(solution)/shard_map/psum | solution.py:49
  300.4 10.3 %multiply_bitcast_fusion = f32[1024,512]{0,1:T(8,128)} fusion(f32[1024,512]{0,1:T(8,128)} %all-reduce.4.cloned.1.call-done, f32[1024,1024]{1,0:T(8,128)} %param.2), kind=kOutput, calls=%fused_computation.1 | convolution fusion | flops 6442975232 | bytes 8388608 | tf_op jit(solution)/shard_map/dot_general | solution.py:31
  310.7 0.0 all-reduce.6.cloned.1.call-update
  310.8 0.0 reduce-scatter.2.cloned.1.call-start
  310.8 102.5 %all-reduce.6.cloned.1.call-done = f32[1024,512]{0,1:T(8,128)} async-done(((f32[1024,512]{0,1:T(8,128)}), f32[1024,512]{0,1:T(8,128)}) %all-reduce.6.cloned.1.call-update) | async-done | bytes 2097168 | tf_op jit(solution)/shard_map/psum | solution.py:52
  413.3 10.3 %convolution_bitcast_fusion = f32[1024,512]{0,1:T(8,128)} fusion(f32[1024,512]{0,1:T(8,128)} %all-reduce.6.cloned.1.call-done, f32[1024,1024]{1,0:T(8,128)} %param.2), kind=kOutput, calls=%fused_computation.4 | convolution fusion | flops 6442450944 | bytes 8388608 | tf_op jit(solution)/shard_map/dot_general | solution.py:42
  423.6 0.0 copy-start
  423.6 0.0 reduce-scatter.2.cloned.1.call-update
  423.6 0.3 all-reduce.8.cloned.1.call-start
  423.9 30.3 %reduce-scatter.2.cloned.1.call-done = f32[1024,128]{0,1:T(8,128)} async-done(((f32[1024,512]{0,1:T(8,128)}), f32[1024,128]{0,1:T(8,128)}) %reduce-scatter.2.cloned.1.call-update) | async-done | bytes 524304 | tf_op jit(solution)/shard_map/reduce_scatter | solution.py:53
  454.2 0.0 copy-done
  454.2 0.0 copy-start.2
  454.2 2.5 fusion.4
  456.7 0.0 all-reduce.8.cloned.1.call-update
  456.7 70.6 %all-reduce.8.cloned.1.call-done = f32[1,128,128]{1,2,0:T(8,128)} async-done(((f32[1,128,128]{1,2,0:T(8,128)}), f32[1,128,128]{1,2,0:T(8,128)}) %all-reduce.8.cloned.1.call-update) | async-done | bytes 65552 | tf_op jit(solution)/shard_map/psum | solution.py:57
  527.3 0.9 copy.6
  528.3 0.9 fusion.7
  529.1 11.7 %custom-call.8 = f32[1,128,128]{2,1,0:T(8,128)S(1)} custom-call(f32[1,128,128]{2,1,0:T(8,128)S(1)} %fusion.7), custom_call_target="Cholesky" | custom-call | tf_op jit(solution)/shard_map/jit(cholesky)/cholesky | solution.py:58
  540.9 0.6 compare_reduce_fusion
  541.5 0.7 fusion.8
  542.2 0.7 copy.8
  542.9 9.8 %custom-call.9 = f32[1,1,128,128]{2,3,1,0:T(8,128)S(1)} custom-call(f32[1,1,128,128]{3,2,1,0:T(8,128)S(1)} %get-tuple-element.5), custom_call_target="InvertDiagBlocksLowerTriangular" | custom-call | tf_op jit(solution)/shard_map/vmap(jit(_solve_triangular))/triangular_solve | solution.py:11
  552.7 0.0 copy-done.2
  552.7 0.6 convolution_bitcast_fusion.1
  553.4 1.0 copy.7
  (1 shorter events, 0.0 us)
Async XLA Ops:
  7.2 27.9 %all-gather.2.cloned.1.call-start = ((), (), s32[]{:S(2)}) async-start(), calls=%async_computation.1 | async-start | bytes 2621440 | tf_op jit(solution)/shard_map/all_gather | solution.py:44
  7.9 292.5 %all-reduce.4.cloned.1.call-start = ((), (), s32[]{:S(2)}) async-start(), calls=%async_computation.2 | async-start | bytes 4194304 | tf_op jit(solution)/shard_map/psum | solution.py:49
  44.3 47.8 %collective-permute-start = (f32[1024,512]{1,0:T(8,128)S(1)}, f32[1024,512]{1,0:T(8,128)S(1)}, u32[]{:S(2)}, u32[]{:S(2)}) collective-permute-start(f32[1024,512]{1,0:T(8,128)S(1)} %convolution_multiply_fusion), channel_id=1, source_target_pairs={{0,4},{4,0},{8,12},{12,8},{16,20},{20,16},{24,28},{28,24},{1,5},{5... | collective-permute-start | bytes 6291464 | tf_op jit(solution)/shard_map/ppermute | solution.py:20
  92.7 50.0 %copy-start.1 = (f32[1024,128]{1,0:T(8,128)S(1)}, f32[1024,128]{1,0:T(8,128)}, u32[]{:S(2)}) copy-start(f32[1024,128]{1,0:T(8,128)} %param.3) | copy-start | bytes 1572868
  92.7 47.0 %collective-permute-start.1 = (f32[1024,512]{1,0:T(8,128)S(1)}, f32[1024,512]{1,0:T(8,128)S(1)}, u32[]{:S(2)}, u32[]{:S(2)}) collective-permute-start(f32[1024,512]{1,0:T(8,128)S(1)} %add.34), channel_id=1, source_target_pairs={{0,8},{4,12},{8,0},{12,4},{16,24},{20,28},{24,16},{28,20},{1,9},{5... | collective-permute-start | bytes 6291464 | tf_op jit(solution)/shard_map/ppermute | solution.py:20
  140.1 92.1 %collective-permute-start.2 = (f32[1024,512]{1,0:T(8,128)S(1)}, f32[1024,512]{1,0:T(8,128)}, u32[]{:S(2)}, u32[]{:S(2)}) collective-permute-start(f32[1024,512]{1,0:T(8,128)S(1)} %add.35), channel_id=1, source_target_pairs={{0,16},{4,20},{8,24},{12,28},{16,0},{20,4},{24,8},{28,12},{1,17},{... | collective-permute-start | bytes 6291464 | tf_op jit(solution)/shard_map/ppermute | solution.py:20
  248.9 164.3 %all-reduce.6.cloned.1.call-start = ((), (), s32[]{:S(2)}) async-start(), calls=%async_computation.3 | async-start | bytes 4194304 | tf_op jit(solution)/shard_map/psum | solution.py:52
  310.8 143.5 %reduce-scatter.2.cloned.1.call-start = ((), (), s32[]{:S(2)}) async-start(), calls=%async_computation.4 | async-start | bytes 2621440 | tf_op jit(solution)/shard_map/reduce_scatter | solution.py:53
  423.6 30.6 %copy-start = (f32[1024,512]{0,1:T(8,128)S(1)}, f32[1024,512]{0,1:T(8,128)}, u32[]{:S(2)}) copy-start(f32[1024,512]{0,1:T(8,128)} %all-reduce.4.cloned.1.call-done) | copy-start | bytes 6291460
  423.6 103.7 %all-reduce.8.cloned.1.call-start = ((), (), s32[]{:S(2)}) async-start(), calls=%async_computation.5 | async-start | bytes 131072 | tf_op jit(solution)/shard_map/psum | solution.py:57
  454.2 98.5 %copy-start.2 = (f32[1024,128]{0,1:T(8,128)S(1)}, f32[1024,128]{0,1:T(8,128)}, u32[]{:S(2)}) copy-start(f32[1024,128]{0,1:T(8,128)} %reduce-scatter.2.cloned.1.call-done) | copy-start | bytes 1572868
Sparse Core Ops, SparseCore 0:
  9.5 25.5 all-gather.1
  249.0 51.3 all-reduce.3
  310.9 102.3 all-reduce.5
  423.7 30.4 reduce-scatter.1
  458.0 69.2 all-reduce.7
